TPU v7x, 256 devices: a whole 4x4x8 slice. The times are simulated.
256 devices in a mesh: layer: 32 (over x, z), row: 2 (over core), col: 4 (over y).
Axes of the slice: x: 4, y: 4, z: 8, core: 2. Of those that a mesh axis runs over, the one named last changes fastest.
Arguments:
- inputs: float32 [1, 4, 384, 128], P(None, 'row', 'col'), may hold values from -6 to 6
- weights: float32 [256, 9, 128, 128], P('layer'), may hold values from -0.1875 to 0.1875
- biases: float32 [256, 128], P('layer'), may hold values from -3 to 3
Outputs:
- states: float32 [256, 1, 4, 384, 128], P('layer', None, 'row', 'col')
All inputs are finite; a program needn't handle non-finite values.
Results may differ from a plain program's by a relative error of at most 0.0003.
Values sent between devices are 32-bit elements; how exact they have to be, the bound alone decides.
A program may use at most 64 MiB of HBM per device.

v0:
```python
import jax
import jax.numpy as jnp
from jax import lax
from jax.experimental import pallas as pl
from jax.experimental.pallas import tpu as pltpu
from jax.sharding import PartitionSpec as P

MESH = pl.DeviceIdType.MESH
F32, BF16 = jnp.float32, jnp.bfloat16
CYCLES = 2
STEP = 0.2
X, Z = 4, 8
CH = 128
LAY = 8
H = 4
TC = 48
TW = TC + 2 * LAY
PX = H * TW
SH = H * TC // Z


def split(a):
    high = a.astype(BF16).astype(F32)
    return high, a - high


def paired(a):
    high, low = split(a)
    return jnp.concatenate([high, low], axis=1).astype(BF16)


def fold(r, m):
    return (r[:m, :CH] + r[:m, CH:]) + (r[m:, :CH] + r[m:, CH:])


def times(a, pair):
    high, low = split(a)
    stacked = jnp.concatenate([high, low], axis=0).astype(BF16)
    r = jnp.dot(stacked, pair, preferred_element_type=F32)
    return fold(r, a.shape[0])


def kernel(
    inp, wts, bias, out,
    xin, x0, wf, wc, psum, a_buf, pad, mask, st, cc, rs, rz, bz, dp, tx, tb, pz, mx, mown, pc, qc, sc, nc, outb,
    s_in, r_in, w_sem, s_sh, r_sh, s_p, r_p, s_pf, r_pf, s_m, r_m, s_a, r_a, s_t, r_t, s_b, r_b,
    s_h, r_h, s_o, r_o, l_o, x_sem,
):
    sec = lax.axis_index("layer")
    r = lax.axis_index("row")
    c = lax.axis_index("col")
    ncol = lax.axis_size("col")
    x, z = sec // Z, sec % Z
    t = 2 * c + r
    last = 2 * ncol - 1

    def at(layer, row, col):
        return {"layer": layer, "row": row, "col": col}

    def remote(src, dst, ss, rr, dev):
        return pltpu.make_async_remote_copy(
            src_ref=src, dst_ref=dst, send_sem=ss, recv_sem=rr, device_id=dev, device_id_type=MESH
        )

    right_rc = (1 - r, c + r)
    left_rc = (1 - r, c - (1 - r))
    has_right, has_left = t < last, t > 0

    load_x = pltpu.make_async_copy(inp.at[0], xin, x_sem.at[0])
    load_x.start()

    def load_w(l):
        return pltpu.make_async_copy(wts.at[l], wf.at[l], w_sem.at[l])

    for l in range(LAY):
        load_w(l).start()

    bar = pltpu.get_barrier_semaphore()

    def greet(dev):
        pl.semaphore_signal(bar, inc=1, device_id=dev, device_id_type=MESH)

    for k in range(1, Z):
        greet(at(x * Z + (z + k) % Z, r, c))
    for k in range(1, X):
        greet(at(((x + k) % X) * Z + z, r, c))

    up = (z == Z - 1) & (x < X - 1)
    down = (z == 0) & (x > 0)

    @pl.when(up)
    def _():
        greet(at(sec + 1, r, c))

    @pl.when(down)
    def _():
        greet(at(sec - 1, r, c))

    for ok, (rr, c2) in ((has_right, right_rc), (has_left, left_rc)):
        @pl.when(ok)
        def _():
            for k in range(Z):
                greet(at(x * Z + k, rr, c2))

            @pl.when(up)
            def _():
                greet(at(sec + 1, rr, c2))

            @pl.when(down)
            def _():
                greet(at(sec - 1, rr, c2))

    @pl.when(c < ncol - 1)
    def _():
        greet(at(sec, r, c + 1))

    @pl.when(c > 0)
    def _():
        greet(at(sec, r, c - 1))

    one = lambda cond: jnp.where(cond, 1, 0)
    sides = one(has_right) + one(has_left)
    peers = (Z - 1) + (X - 1) + sides * Z + (1 + sides) * (one(up) + one(down)) + one(c < ncol - 1) + one(c > 0)

    zero_cols = jnp.zeros((H, LAY, CH), F32)

    @pl.when(t == 0)
    def _():
        x0[:, 0:LAY, :] = zero_cols
        for i in range(CYCLES):
            st[i, :, 0:LAY, :] = zero_cols
            dp[i, :, 0:LAY, :] = zero_cols

    @pl.when(t == last)
    def _():
        x0[:, TW - LAY : TW, :] = zero_cols
        for i in range(CYCLES):
            st[i, :, TW - LAY : TW, :] = zero_cols
            dp[i, :, TW - LAY : TW, :] = zero_cols

    a_buf[...] = jnp.zeros_like(a_buf)
    pad[...] = jnp.zeros_like(pad)
    psum[...] = jnp.zeros_like(psum)
    column = lax.broadcasted_iota(jnp.int32, (H, TW, CH), 1)
    inside = ((column >= LAY) | (t > 0)) & ((column < TW - LAY) | (t < last))
    mask[...] = jnp.where(inside, 1.0, 0.0).astype(F32).reshape(PX, CH)

    pl.semaphore_wait(bar, peers)
    load_x.wait()

    wide = TC + LAY
    half = pl.ds(2 * r, 2)
    mine = pl.ds(pl.multiple_of(LAY * (1 - r), LAY), wide)
    theirs = pl.ds(pl.multiple_of(LAY * r, LAY), wide)
    src_mine = pl.ds(pl.multiple_of((TC - LAY) * r, LAY), wide)
    src_theirs = pl.ds(pl.multiple_of((TC - LAY) * (1 - r), LAY), wide)
    to_core = remote(xin.at[:, src_theirs, :], x0.at[half, theirs, :], s_in.at[0], r_in.at[0], at(sec, 1 - r, c))
    to_right = remote(
        xin.at[:, pl.ds(2 * TC - LAY, LAY), :], x0.at[half, pl.ds(0, LAY), :], s_in.at[1], r_in.at[1 + r], at(sec, 0, c + 1)
    )
    to_left = remote(
        xin.at[:, pl.ds(0, LAY), :], x0.at[half, pl.ds(TW - LAY, LAY), :], s_in.at[2], r_in.at[3 + r], at(sec, 1, c - 1)
    )
    to_core.start()

    @pl.when(c < ncol - 1)
    def _():
        to_right.start()

    @pl.when(c > 0)
    def _():
        to_left.start()

    x0[half, mine, :] = xin[:, src_mine, :]

    def got_in(i, cols):
        part = x0.at[pl.ds(0, 2), cols, :]
        return remote(part, part, s_in.at[0], r_in.at[i], at(sec, 1 - r, c))

    got_in(0, pl.ds(0, wide)).wait_recv()

    @pl.when((r == 0) & (c > 0))
    def _():
        got_in(1, pl.ds(0, LAY)).wait_recv()
        got_in(2, pl.ds(0, LAY)).wait_recv()

    @pl.when((r == 1) & (c < ncol - 1))
    def _():
        got_in(3, pl.ds(0, LAY)).wait_recv()
        got_in(4, pl.ds(0, LAY)).wait_recv()

    to_core.wait_send()

    @pl.when(c < ncol - 1)
    def _():
        to_right.wait_send()

    @pl.when(c > 0)
    def _():
        to_left.wait_send()

    def set_start(value):
        pad[LAY : LAY + PX, :] = value.reshape(PX, CH)

    def layer(l):
        v = pad[LAY : LAY + PX, :]
        for d in range(3):
            high, low = split(pad[LAY - 1 + d : LAY - 1 + d + PX, :])
            a_buf[0, TW : TW + PX, d * CH : (d + 1) * CH] = high.astype(BF16)
            a_buf[1, TW : TW + PX, d * CH : (d + 1) * CH] = low.astype(BF16)
        lhs = jnp.concatenate(
            [
                jnp.concatenate([a_buf[h, d * TW : d * TW + PX, :] for d in range(3)], axis=1)
                for h in range(2)
            ],
            axis=0,
        )
        pre = fold(jnp.dot(lhs, wc[l], preferred_element_type=F32), PX)
        new = (v + STEP * jnp.tanh(pre + bias[pl.ds(l, 1), :])) * mask[...]
        pad[LAY : LAY + PX, :] = new
        return new

    def core(value):
        return value.reshape(H, TW, CH)[:, LAY : LAY + TC, :]

    set_start(x0[...])

    def first(l, carry):
        load_w(l).wait()
        total = psum[...]
        for k in range(9):
            w = wf[l, k]
            total = total + w
            wc[l, k * CH : (k + 1) * CH, :] = paired(w)
        psum[...] = total
        layer(l)
        return carry

    def plain(l, carry):
        layer(l)
        return carry

    lax.fori_loop(0, LAY, first, 0)
    rows_i = lax.broadcasted_iota(jnp.int32, (CH, CH), 0)
    cols_i = lax.broadcasted_iota(jnp.int32, (CH, CH), 1)
    eye = jnp.where(rows_i == cols_i, 1.0, 0.0).astype(F32)
    psum[...] = eye + STEP * psum[...]

    def shift(i):
        nxt = sec + 1
        main = remote(cc.at[i], st.at[i, :, pl.ds(LAY, TC), :], s_sh.at[i, 0], r_sh.at[i, 0], at(nxt, r, c))
        rgt = remote(
            cc.at[i, :, pl.ds(TC - LAY, LAY), :], st.at[i, :, pl.ds(0, LAY), :], s_sh.at[i, 1], r_sh.at[i, 1], at(nxt, *right_rc)
        )
        lft = remote(
            cc.at[i, :, pl.ds(0, LAY), :], st.at[i, :, pl.ds(TW - LAY, LAY), :], s_sh.at[i, 2], r_sh.at[i, 2], at(nxt, *left_rc)
        )
        return main, rgt, lft

    def shift_send(i):
        main, rgt, lft = shift(i)

        @pl.when(sec < X * Z - 1)
        def _():
            @pl.when(has_right)
            def _():
                rgt.start()

            @pl.when(has_left)
            def _():
                lft.start()

            main.start()

    def shift_wait(i):
        main, rgt, lft = shift(i)

        @pl.when(sec > 0)
        def _():
            main.wait_recv()

            @pl.when(has_left)
            def _():
                rgt.wait_recv()

            @pl.when(has_right)
            def _():
                lft.wait_recv()

        @pl.when(sec == 0)
        def _():
            st[i] = x0[...]

        @pl.when(sec < X * Z - 1)
        def _():
            main.wait_send()

            @pl.when(has_right)
            def _():
                rgt.wait_send()

            @pl.when(has_left)
            def _():
                lft.wait_send()

    hrows = pl.ds(pl.multiple_of(r * (CH // 2), CH // 2), CH // 2)

    def p_copy(k):
        return remote(
            psum.at[hrows, :], pz.at[z, hrows, :], s_p.at[k], r_p.at[k], at(x * Z + (z + k) % Z, r, c)
        )

    def m_copy(k):
        return remote(mown, mx.at[x], s_m.at[k], r_m.at[k], at(((x + k) % X) * Z + z, r, c))

    def a_copy(i, k):
        j = (z + k) % Z
        part = rs.at[i, j // 2, pl.ds(pl.multiple_of(SH * (j % 2), LAY), SH), :]
        return remote(part, rz.at[i, z], s_a.at[i, k], r_a.at[i, k], at(x * Z + j, r, c))

    def t_copy(i, k):
        return remote(tb.at[i], tx.at[i, x], s_t.at[i, k], r_t.at[i, k], at(((x + k) % X) * Z + z, r, c))

    my_cols = pl.ds(pl.multiple_of(LAY + SH * (z % 2), LAY), SH)

    def b_copy(i, k):
        j = (z + k) % Z
        return remote(bz.at[i, j], dp.at[i, z // 2, my_cols, :], s_b.at[i, k], r_b.at[i, k], at(x * Z + j, r, c))

    def h_copy(i, k, side):
        frm = (SH - LAY) if side == 0 else 0
        to = 0 if side == 0 else TW - LAY
        rc = right_rc if side == 0 else left_rc
        return remote(
            bz.at[i, k, pl.ds(frm, LAY), :], dp.at[i, z // 2, pl.ds(to, LAY), :], s_h.at[i, k], r_h.at[i, side, z // 2],
            at(x * Z + k, *rc),
        )

    my_shard = (z // 2, pl.ds(pl.multiple_of(SH * (z % 2), LAY), SH))

    for i in range(CYCLES):
        if i > 0:
            lax.fori_loop(0, LAY, plain, 0)
        cc[i] = core(pad[LAY : LAY + PX, :])
        shift_send(i)
        if i == 0:
            for k in range(1, Z):
                p_copy(k).start()
            pz[z, hrows, :] = psum[hrows, :]
        shift_wait(i)
        set_start(st[i])
        lax.fori_loop(0, LAY, plain, 0)
        rs[i] = core(pad[LAY : LAY + PX, :]) - cc[i]
        for k in (4, 3, 5, 2, 6, 1, 7):
            a_copy(i, k).start()
        rz[i, z] = rs[i, my_shard[0], my_shard[1], :]
        if i == 0:
            for k in range(1, Z):
                p_copy(k).wait()
            forward = remote(pz.at[:, hrows, :], pz.at[:, hrows, :], s_pf.at[0], r_pf.at[0], at(sec, 1 - r, c))
            forward.start()
            forward.wait()
            prefix, suffix = pz[0], eye
            for k in range(Z):
                pc[k] = paired(pz[k])
            for k in range(Z):
                if k > 0:
                    prefix = times(prefix, pc[k])
                if k < Z - 1:
                    qc[:, 2 * CH * k : 2 * CH * (k + 1)] = paired(prefix)
                back = Z - 1 - k
                pair = paired(suffix)
                sc[back * CH : (back + 1) * CH, :] = pair
                if back > 0:
                    suffix = times(pz[back], pair)
            mown[...] = prefix
            for k in range(1, X):
                m_copy(k).start()
        for k in range(1, Z):
            a_copy(i, k).wait()
        joined = jnp.concatenate([rz[i, k] for k in range(Z)], axis=1)
        tb[i] = times(joined, sc[...])
        for k in range(1, X):
            t_copy(i, k).start()
        run = rz[i, 0]
        local = [run]
        for k in range(1, Z - 1):
            run = times(run, pc[k]) + rz[i, k]
            local.append(run)
        if i == 0:
            for k in range(1, X):
                m_copy(k).wait()
            near = mx[jnp.maximum(x - 1, 0)]
            far = mx[jnp.maximum(x - 2, 0)]
            near = jnp.where(x >= 2, near, 0.0)
            far = jnp.where(x >= 3, far, 0.0)
            near_pair = paired(near)
            nc[0:CH, :] = near_pair
            nc[CH : 2 * CH, :] = paired(times(far, near_pair))
        for k in range(1, X):
            t_copy(i, k).wait()
        before = [jnp.where(x >= d, tx[i, jnp.maximum(x - d, 0)], 0.0) for d in range(1, X)]
        carry = before[0] + times(jnp.concatenate(before[1:], axis=1), nc[...])
        bz[i, 0] = carry
        high, low = split(carry)
        spread = jnp.dot(jnp.concatenate([high, low], axis=0).astype(BF16), qc[...], preferred_element_type=F32)
        for k in range(1, Z):
            bz[i, k] = local[k - 1] + fold(spread[:, 2 * CH * (k - 1) : 2 * CH * k], SH)
        for k in (4, 3, 5, 2, 6, 1, 7):
            b_copy(i, k).start()

        @pl.when((z % 2 == 1) & has_right)
        def _():
            for k in range(Z):
                h_copy(i, k, 0).start()

        @pl.when((z % 2 == 0) & has_left)
        def _():
            for k in range(Z):
                h_copy(i, k, 1).start()

        dp[i, z // 2, my_cols, :] = bz[i, z]
        for k in range(1, Z):
            b_copy(i, k).wait()

        def halo_in(side, row):
            part = dp.at[i, row, pl.ds(0 if side == 0 else TW - LAY, LAY), :]
            return remote(part, part, s_h.at[i, 0], r_h.at[i, side, row], at(sec, 1 - r, c))

        @pl.when(has_left)
        def _():
            for row in range(H):
                halo_in(0, row).wait_recv()

        @pl.when(has_right)
        def _():
            for row in range(H):
                halo_in(1, row).wait_recv()

        @pl.when((z % 2 == 1) & has_right)
        def _():
            for k in range(Z):
                h_copy(i, k, 0).wait_send()

        @pl.when((z % 2 == 0) & has_left)
        def _():
            for k in range(Z):
                h_copy(i, k, 1).wait_send()

        set_start(st[i] + dp[i])

    out_cols = pl.ds(pl.multiple_of(TC * r, LAY), TC)

    def keep(l):
        return pltpu.make_async_copy(outb.at[l, half], out.at[l, 0, :, out_cols, :], l_o.at[l])

    def give(l):
        return remote(
            outb.at[l, pl.ds(2 * (1 - r), 2)], out.at[l, 0, :, out_cols, :], s_o.at[l], r_o.at[l], at(sec, 1 - r, c)
        )

    i = CYCLES - 1
    delta = times(dp[i, :, pl.ds(LAY, TC), :].reshape(H * TC, CH), paired(psum[...])).reshape(H, TC, CH) + rs[i]
    outb[LAY - 1] = cc[i] + delta
    keep(LAY - 1).start()
    give(LAY - 1).start()

    def final(l, carry):
        outb[l] = core(layer(l))
        keep(l).start()
        give(l).start()
        return carry

    lax.fori_loop(0, LAY - 1, final, 0)
    for l in range(LAY):
        keep(l).wait()
        give(l).wait()


def shards(inputs, weights, biases):
    V, D = pltpu.VMEM, pltpu.SemaphoreType.DMA
    rows, cols = inputs.shape[1], inputs.shape[2]
    n = CYCLES
    return pl.pallas_call(
        kernel,
        out_shape=jax.ShapeDtypeStruct((LAY,) + inputs.shape, F32),
        in_specs=[
            pl.BlockSpec(memory_space=pl.ANY),
            pl.BlockSpec(memory_space=pl.ANY),
            pl.BlockSpec(memory_space=pltpu.VMEM),
        ],
        out_specs=pl.BlockSpec(memory_space=pl.ANY),
        scratch_shapes=[
            V((rows, cols, CH), F32),
            V((H, TW, CH), F32),
            V((LAY, 9, CH, CH), F32),
            V((LAY, 9 * CH, 2 * CH), BF16),
            V((CH, CH), F32),
            V((2, PX + 2 * TW, 3 * CH), BF16),
            V((PX + 2 * LAY, CH), F32),
            V((PX, CH), F32),
            V((n, H, TW, CH), F32),
            V((n, H, TC, CH), F32),
            V((n, H, TC, CH), F32),
            V((n, Z, SH, CH), F32),
            V((n, Z, SH, CH), F32),
            V((n, H, TW, CH), F32),
            V((n, X, SH, CH), F32),
            V((n, SH, CH), F32),
            V((Z, CH, CH), F32),
            V((X, CH, CH), F32),
            V((CH, CH), F32),
            V((Z, CH, 2 * CH), BF16),
            V((CH, 2 * CH * (Z - 1)), BF16),
            V((Z * CH, 2 * CH), BF16),
            V((2 * CH, 2 * CH), BF16),
            V((LAY, H, TC, CH), F32),
            D((3,)), D((5,)), D((LAY,)), D((n, 3)), D((n, 3)), D((Z,)), D((Z,)), D((1,)), D((1,)),
            D((X,)), D((X,)), D((n, Z)), D((n, Z)), D((n, X)), D((n, X)), D((n, Z)), D((n, Z)),
            D((n, Z)), D((n, 2, H)), D((LAY,)), D((LAY,)), D((LAY,)), D((1,)),
        ],
        compiler_params=pltpu.CompilerParams(
            collective_id=0, has_side_effects=True, vmem_limit_bytes=48 * 1024 * 1024
        ),
    )(inputs, weights, biases)


def solution(mesh):
    return jax.shard_map(
        shards,
        mesh=mesh,
        in_specs=(P(None, "row", "col", None), P("layer", None, None, None), P("layer", None)),
        out_specs=P("layer", None, "row", "col", None),
        check_vma=False,
    )
```

profile of v0, /device:TPU:1, one launch (start us, length us, event | category | flops | bytes accessed | tf_op | source)
XLA Modules:
  0.0 83.8 jit_solution(12027620574902808350)
XLA Ops:
  0.0 0.0 copy-start
  0.0 2.3 %copy-done = f32[8,9,128,128]{3,2,1,0:T(8,128)S(1)} copy-done((f32[8,9,128,128]{3,2,1,0:T(8,128)S(1)}, f32[8,9,128,128]{3,2,1,0:T(8,128)}, u32[]{:S(2)}) %copy-start) | copy-done | bytes 4718616
  2.3 0.0 copy-start.1
  2.3 0.9 %copy-done.1 = f32[1,2,96,128]{3,2,1,0:T(8,128)S(1)} copy-done((f32[1,2,96,128]{3,2,1,0:T(8,128)S(1)}, f32[1,2,96,128]{3,2,1,0:T(8,128)}, u32[]{:S(2)}) %copy-start.1) | copy-done | bytes 98328
  3.2 0.0 copy-start.2
  3.2 0.7 copy-done.2
  3.9 79.0 %shard_map.37 = f32[8,1,2,96,128]{4,3,2,1,0:T(8,128)S(1)} custom-call(f32[1,2,96,128]{3,2,1,0:T(8,128)S(1)} %copy-done.1, f32[8,9,128,128]{3,2,1,0:T(8,128)S(1)} %copy-done, f32[8,128]{1,0:T(8,128)S(1)} %copy-done.2), custom_call_target="tpu_custom_call" | custom-call | tf_op jit(solution)/shard_map/pallas_call | solution.py:484
  82.9 0.9 %copy.5 = f32[8,1,2,96,128]{4,3,2,1,0:T(8,128)} copy(f32[8,1,2,96,128]{4,3,2,1,0:T(8,128)S(1)} %shard_map.37) | data formatting | bytes 1572864
Async XLA Ops:
  0.0 2.3 %copy-start = (f32[8,9,128,128]{3,2,1,0:T(8,128)S(1)}, f32[8,9,128,128]{3,2,1,0:T(8,128)}, u32[]{:S(2)}) copy-start(f32[8,9,128,128]{3,2,1,0:T(8,128)} %wts.1) | copy-start | bytes 14155780
  2.3 0.9 %copy-start.1 = (f32[1,2,96,128]{3,2,1,0:T(8,128)S(1)}, f32[1,2,96,128]{3,2,1,0:T(8,128)}, u32[]{:S(2)}) copy-start(f32[1,2,96,128]{3,2,1,0:T(8,128)} %inp.1) | copy-start | bytes 294916
  3.2 0.7 copy-start.2
where the time goes:
time: 84 us; the launch traced here: 83.8 us
  Pallas kernels  79 us (94%)
  local copies, waits for them, and re-layouts  4.8 us (6%)
    pallas_call x1, Pallas kernels, shards(): pl.pallas_call(kernel, out_shape=jax.ShapeDtypeStruct((LAY,) + inputs.sha...  79 us
    unnamed x7, local copies, waits for them, and re-layouts  4.8 us

commit v1 on v0

--- a/solution.py
+++ b/solution.py
@@ -41,8 +41,8 @@
 
 
 def kernel(
-    inp, wts, bias, out,
-    xin, x0, wf, wc, psum, a_buf, pad, mask, st, cc, rs, rz, bz, dp, tx, tb, pz, mx, mown, pc, qc, sc, nc, outb,
+    inp, wts, bias_in, out,
+    xin, bias, x0, wf, wc, psum, a_buf, pad, mask, st, cc, rs, rz, bz, dp, tx, tb, pz, mx, mown, pc, qc, sc, nc, outb,
     s_in, r_in, w_sem, s_sh, r_sh, s_p, r_p, s_pf, r_pf, s_m, r_m, s_a, r_a, s_t, r_t, s_b, r_b,
     s_h, r_h, s_o, r_o, l_o, x_sem,
 ):
@@ -68,6 +68,8 @@
 
     load_x = pltpu.make_async_copy(inp.at[0], xin, x_sem.at[0])
     load_x.start()
+    load_b = pltpu.make_async_copy(bias_in, bias, x_sem.at[1])
+    load_b.start()
 
     def load_w(l):
         return pltpu.make_async_copy(wts.at[l], wf.at[l], w_sem.at[l])
@@ -145,8 +147,24 @@
     inside = ((column >= LAY) | (t > 0)) & ((column < TW - LAY) | (t < last))
     mask[...] = jnp.where(inside, 1.0, 0.0).astype(F32).reshape(PX, CH)
 
+    def convert(l, carry):
+        load_w(l).wait()
+        total = psum[...]
+        for k in range(9):
+            w = wf[l, k]
+            total = total + w
+            wc[l, k * CH : (k + 1) * CH, :] = paired(w)
+        psum[...] = total
+        return carry
+
+    lax.fori_loop(0, LAY, convert, 0)
+    rows_i = lax.broadcasted_iota(jnp.int32, (CH, CH), 0)
+    cols_i = lax.broadcasted_iota(jnp.int32, (CH, CH), 1)
+    eye = jnp.where(rows_i == cols_i, 1.0, 0.0).astype(F32)
+    psum[...] = eye + STEP * psum[...]
+    load_x.wait()
+    load_b.wait()
     pl.semaphore_wait(bar, peers)
-    load_x.wait()
 
     wide = TC + LAY
     half = pl.ds(2 * r, 2)
@@ -171,6 +189,16 @@
     def _():
         to_left.start()
 
+    hrows = pl.ds(pl.multiple_of(r * (CH // 2), CH // 2), CH // 2)
+
+    def p_copy(k):
+        return remote(
+            psum.at[hrows, :], pz.at[z, hrows, :], s_p.at[k], r_p.at[k], at(x * Z + (z + k) % Z, r, c)
+        )
+
+    for k in (4, 3, 5, 2, 6, 1, 7):
+        p_copy(k).start()
+    pz[z, hrows, :] = psum[hrows, :]
     x0[half, mine, :] = xin[:, src_mine, :]
 
     def got_in(i, cols):
@@ -225,26 +253,9 @@
 
     set_start(x0[...])
 
-    def first(l, carry):
-        load_w(l).wait()
-        total = psum[...]
-        for k in range(9):
-            w = wf[l, k]
-            total = total + w
-            wc[l, k * CH : (k + 1) * CH, :] = paired(w)
-        psum[...] = total
-        layer(l)
-        return carry
-
     def plain(l, carry):
         layer(l)
         return carry
-
-    lax.fori_loop(0, LAY, first, 0)
-    rows_i = lax.broadcasted_iota(jnp.int32, (CH, CH), 0)
-    cols_i = lax.broadcasted_iota(jnp.int32, (CH, CH), 1)
-    eye = jnp.where(rows_i == cols_i, 1.0, 0.0).astype(F32)
-    psum[...] = eye + STEP * psum[...]
 
     def shift(i):
         nxt = sec + 1
@@ -302,13 +313,6 @@
             @pl.when(has_left)
             def _():
                 lft.wait_send()
-
-    hrows = pl.ds(pl.multiple_of(r * (CH // 2), CH // 2), CH // 2)
-
-    def p_copy(k):
-        return remote(
-            psum.at[hrows, :], pz.at[z, hrows, :], s_p.at[k], r_p.at[k], at(x * Z + (z + k) % Z, r, c)
-        )
 
     def m_copy(k):
         return remote(mown, mx.at[x], s_m.at[k], r_m.at[k], at(((x + k) % X) * Z + z, r, c))
@@ -339,21 +343,9 @@
     my_shard = (z // 2, pl.ds(pl.multiple_of(SH * (z % 2), LAY), SH))
 
     for i in range(CYCLES):
-        if i > 0:
-            lax.fori_loop(0, LAY, plain, 0)
+        lax.fori_loop(0, LAY, plain, 0)
         cc[i] = core(pad[LAY : LAY + PX, :])
         shift_send(i)
-        if i == 0:
-            for k in range(1, Z):
-                p_copy(k).start()
-            pz[z, hrows, :] = psum[hrows, :]
-        shift_wait(i)
-        set_start(st[i])
-        lax.fori_loop(0, LAY, plain, 0)
-        rs[i] = core(pad[LAY : LAY + PX, :]) - cc[i]
-        for k in (4, 3, 5, 2, 6, 1, 7):
-            a_copy(i, k).start()
-        rz[i, z] = rs[i, my_shard[0], my_shard[1], :]
         if i == 0:
             for k in range(1, Z):
                 p_copy(k).wait()
@@ -376,6 +368,23 @@
             mown[...] = prefix
             for k in range(1, X):
                 m_copy(k).start()
+        shift_wait(i)
+        set_start(st[i])
+        lax.fori_loop(0, LAY, plain, 0)
+        rs[i] = core(pad[LAY : LAY + PX, :]) - cc[i]
+        for k in (4, 3, 5, 2, 6, 1, 7):
+            a_copy(i, k).start()
+        rz[i, z] = rs[i, my_shard[0], my_shard[1], :]
+        if i == 0:
+            for k in range(1, X):
+                m_copy(k).wait()
+            near = mx[jnp.maximum(x - 1, 0)]
+            far = mx[jnp.maximum(x - 2, 0)]
+            near = jnp.where(x >= 2, near, 0.0)
+            far = jnp.where(x >= 3, far, 0.0)
+            near_pair = paired(near)
+            nc[0:CH, :] = near_pair
+            nc[CH : 2 * CH, :] = paired(times(far, near_pair))
         for k in range(1, Z):
             a_copy(i, k).wait()
         joined = jnp.concatenate([rz[i, k] for k in range(Z)], axis=1)
@@ -387,16 +396,6 @@
         for k in range(1, Z - 1):
             run = times(run, pc[k]) + rz[i, k]
             local.append(run)
-        if i == 0:
-            for k in range(1, X):
-                m_copy(k).wait()
-            near = mx[jnp.maximum(x - 1, 0)]
-            far = mx[jnp.maximum(x - 2, 0)]
-            near = jnp.where(x >= 2, near, 0.0)
-            far = jnp.where(x >= 3, far, 0.0)
-            near_pair = paired(near)
-            nc[0:CH, :] = near_pair
-            nc[CH : 2 * CH, :] = paired(times(far, near_pair))
         for k in range(1, X):
             t_copy(i, k).wait()
         before = [jnp.where(x >= d, tx[i, jnp.maximum(x - d, 0)], 0.0) for d in range(1, X)]
@@ -485,13 +484,14 @@
         kernel,
         out_shape=jax.ShapeDtypeStruct((LAY,) + inputs.shape, F32),
         in_specs=[
-            pl.BlockSpec(memory_space=pl.ANY),
-            pl.BlockSpec(memory_space=pl.ANY),
-            pl.BlockSpec(memory_space=pltpu.VMEM),
+            pl.BlockSpec(memory_space=pltpu.HBM),
+            pl.BlockSpec(memory_space=pltpu.HBM),
+            pl.BlockSpec(memory_space=pltpu.HBM),
         ],
         out_specs=pl.BlockSpec(memory_space=pl.ANY),
         scratch_shapes=[
             V((rows, cols, CH), F32),
+            V((LAY, CH), F32),
             V((H, TW, CH), F32),
             V((LAY, 9, CH, CH), F32),
             V((LAY, 9 * CH, 2 * CH), BF16),
@@ -517,10 +517,10 @@
             V((LAY, H, TC, CH), F32),
             D((3,)), D((5,)), D((LAY,)), D((n, 3)), D((n, 3)), D((Z,)), D((Z,)), D((1,)), D((1,)),
             D((X,)), D((X,)), D((n, Z)), D((n, Z)), D((n, X)), D((n, X)), D((n, Z)), D((n, Z)),
-            D((n, Z)), D((n, 2, H)), D((LAY,)), D((LAY,)), D((LAY,)), D((1,)),
+            D((n, Z)), D((n, 2, H)), D((LAY,)), D((LAY,)), D((LAY,)), D((2,)),
         ],
         compiler_params=pltpu.CompilerParams(
-            collective_id=0, has_side_effects=True, vmem_limit_bytes=48 * 1024 * 1024
+            collective_id=0, has_side_effects=True, vmem_limit_bytes=63000000
         ),
     )(inputs, weights, biases)
 

time: 84 us -> 79.1 us (0.942)
  local copies, waits for them, and re-layouts: 4.8 us -> 2.07 us
  Pallas kernels: 79 us -> 76.9 us
    unnamed x7 -> x1, local copies, waits for them, and re-layouts: 4.8 us -> 2.07 us
    pallas_call x1, Pallas kernels: 79 us -> 76.9 us  [shards(): pl.pallas_call(kernel, out_shape=jax.ShapeDtypeStruct((LAY,) + inputs.sha...]
where the time goes in v1:
time: 79.1 us; the launch traced here: 79 us
  Pallas kernels  76.9 us (97%)
  local copies, waits for them, and re-layouts  2.07 us (3%)
    pallas_call x1, Pallas kernels, shards(): pl.pallas_call(kernel, out_shape=jax.ShapeDtypeStruct((LAY,) + inputs.sha...  76.9 us
    unnamed x1, local copies, waits for them, and re-layouts  2.07 us

profile of v1, /device:TPU:1, one launch (start us, length us, event | category | flops | bytes accessed | tf_op | source)
XLA Modules:
  0.0 79.0 jit_solution(3406413504456354434)
XLA Ops:
  0.0 76.9 %shard_map.37 = f32[8,1,2,96,128]{4,3,2,1,0:T(8,128)} custom-call(f32[1,2,96,128]{3,2,1,0:T(8,128)} %inp.1, f32[8,9,128,128]{3,2,1,0:T(8,128)} %wts.1, f32[8,128]{1,0:T(8,128)} %bias_in.1), custom_call_target="tpu_custom_call" | custom-call | tf_op jit(solution)/shard_map/pallas_call | solution.py:483
  76.9 2.1 %copy.5 = f32[8,1,2,96,128]{4,3,2,1,0:T(8,128)} copy(f32[8,1,2,96,128]{4,3,2,1,0:T(8,128)} %shard_map.37) | data formatting | bytes 1572864

commit v2 on v1

--- a/solution.py
+++ b/solution.py
@@ -44,7 +44,7 @@
     inp, wts, bias_in, out,
     xin, bias, x0, wf, wc, psum, a_buf, pad, mask, st, cc, rs, rz, bz, dp, tx, tb, pz, mx, mown, pc, qc, sc, nc, outb,
     s_in, r_in, w_sem, s_sh, r_sh, s_p, r_p, s_pf, r_pf, s_m, r_m, s_a, r_a, s_t, r_t, s_b, r_b,
-    s_h, r_h, s_o, r_o, l_o, x_sem,
+    s_h, r_h, s_o, r_o, l_o, x_sem, s_y, r_y, rounds,
 ):
     sec = lax.axis_index("layer")
     r = lax.axis_index("row")
@@ -82,47 +82,39 @@
     def greet(dev):
         pl.semaphore_signal(bar, inc=1, device_id=dev, device_id_type=MESH)
 
-    for k in range(1, Z):
-        greet(at(x * Z + (z + k) % Z, r, c))
-    for k in range(1, X):
-        greet(at(((x + k) % X) * Z + z, r, c))
-
-    up = (z == Z - 1) & (x < X - 1)
-    down = (z == 0) & (x > 0)
-
-    @pl.when(up)
-    def _():
-        greet(at(sec + 1, r, c))
-
-    @pl.when(down)
-    def _():
-        greet(at(sec - 1, r, c))
-
-    for ok, (rr, c2) in ((has_right, right_rc), (has_left, left_rc)):
-        @pl.when(ok)
-        def _():
-            for k in range(Z):
-                greet(at(x * Z + k, rr, c2))
-
-            @pl.when(up)
-            def _():
-                greet(at(sec + 1, rr, c2))
-
-            @pl.when(down)
-            def _():
-                greet(at(sec - 1, rr, c2))
-
-    @pl.when(c < ncol - 1)
-    def _():
-        greet(at(sec, r, c + 1))
-
-    @pl.when(c > 0)
-    def _():
-        greet(at(sec, r, c - 1))
+    up_rc, down_rc = at(sec, r, c + 1), at(sec, r, c - 1)
+    around = [at(x * Z + (z + d) % Z, r, c) for d in (1, Z - 1)] + [at(((x + d) % X) * Z + z, r, c) for d in (1, X - 1)]
+    for dev in around + [at(sec, 1 - r, c)]:
+        greet(dev)
+    has_next, has_prev = c < ncol - 1, c > 0
+
+    @pl.when(has_next)
+    def _():
+        greet(up_rc)
+        greet(at(sec, 1 - r, c + 1))
+
+    @pl.when(has_prev)
+    def _():
+        greet(down_rc)
+        greet(at(sec, 1 - r, c - 1))
 
     one = lambda cond: jnp.where(cond, 1, 0)
-    sides = one(has_right) + one(has_left)
-    peers = (Z - 1) + (X - 1) + sides * Z + (1 + sides) * (one(up) + one(down)) + one(c < ncol - 1) + one(c > 0)
+    sides = one(has_next) + one(has_prev)
+
+    def tell(k):
+        for dev in around:
+            pl.semaphore_signal(rounds.at[k], inc=1, device_id=dev, device_id_type=MESH)
+
+        @pl.when(has_next)
+        def _():
+            pl.semaphore_signal(rounds.at[k], inc=1, device_id=up_rc, device_id_type=MESH)
+
+        @pl.when(has_prev)
+        def _():
+            pl.semaphore_signal(rounds.at[k], inc=1, device_id=down_rc, device_id_type=MESH)
+
+    def hear(k):
+        pl.semaphore_wait(rounds.at[k], len(around) + sides)
 
     zero_cols = jnp.zeros((H, LAY, CH), F32)
 
@@ -157,14 +149,10 @@
         psum[...] = total
         return carry
 
-    lax.fori_loop(0, LAY, convert, 0)
-    rows_i = lax.broadcasted_iota(jnp.int32, (CH, CH), 0)
-    cols_i = lax.broadcasted_iota(jnp.int32, (CH, CH), 1)
-    eye = jnp.where(rows_i == cols_i, 1.0, 0.0).astype(F32)
-    psum[...] = eye + STEP * psum[...]
+    lax.fori_loop(0, 3, convert, 0)
     load_x.wait()
     load_b.wait()
-    pl.semaphore_wait(bar, peers)
+    pl.semaphore_wait(bar, len(around) + 1 + 2 * sides)
 
     wide = TC + LAY
     half = pl.ds(2 * r, 2)
@@ -190,16 +178,31 @@
         to_left.start()
 
     hrows = pl.ds(pl.multiple_of(r * (CH // 2), CH // 2), CH // 2)
+    slab = CH // 8
+    prows = pl.ds(pl.multiple_of(slab * (4 * r + c), slab), slab)
 
     def p_copy(k):
         return remote(
-            psum.at[hrows, :], pz.at[z, hrows, :], s_p.at[k], r_p.at[k], at(x * Z + (z + k) % Z, r, c)
-        )
-
-    for k in (4, 3, 5, 2, 6, 1, 7):
-        p_copy(k).start()
-    pz[z, hrows, :] = psum[hrows, :]
+            psum.at[prows, :], pz.at[z, prows, :], s_p.at[k], r_p.at[k], at(x * Z + (z + k) % Z, r, c)
+        )
+
+    def y_copy(k):
+        part = pz.at[:, prows, :]
+        return remote(part, part, s_y.at[k], r_y.at[k], at(sec, r, (c + k) % 4))
+
+    tell(0)
     x0[half, mine, :] = xin[:, src_mine, :]
+    lax.fori_loop(3, 5, convert, 0)
+    hear(0)
+    tell(1)
+    lax.fori_loop(5, LAY, convert, 0)
+    rows_i = lax.broadcasted_iota(jnp.int32, (CH, CH), 0)
+    cols_i = lax.broadcasted_iota(jnp.int32, (CH, CH), 1)
+    eye = jnp.where(rows_i == cols_i, 1.0, 0.0).astype(F32)
+    psum[...] = eye + STEP * psum[...]
+    pz[z, prows, :] = psum[prows, :]
+    hear(1)
+    tell(2)
 
     def got_in(i, cols):
         part = x0.at[pl.ds(0, 2), cols, :]
@@ -236,14 +239,22 @@
             high, low = split(pad[LAY - 1 + d : LAY - 1 + d + PX, :])
             a_buf[0, TW : TW + PX, d * CH : (d + 1) * CH] = high.astype(BF16)
             a_buf[1, TW : TW + PX, d * CH : (d + 1) * CH] = low.astype(BF16)
-        lhs = jnp.concatenate(
-            [
-                jnp.concatenate([a_buf[h, d * TW : d * TW + PX, :] for d in range(3)], axis=1)
-                for h in range(2)
-            ],
-            axis=0,
-        )
-        pre = fold(jnp.dot(lhs, wc[l], preferred_element_type=F32), PX)
+        def both(lo, hi, cols):
+            return jnp.concatenate([a_buf[h, lo:hi, cols] for h in range(2)], axis=0)
+
+        rows3 = PX - TW
+        pair, third = slice(0, 2 * CH), slice(2 * CH, 3 * CH)
+        mid = jnp.concatenate(
+            [both(TW, TW + PX, pair), both(TW, TW + PX, third), both(0, PX, third)], axis=1
+        )
+        w_mid = jnp.concatenate([wc[l, 3 * CH : 6 * CH, :], wc[l, 2 * CH : 3 * CH, :]], axis=0)
+        full = fold(jnp.dot(mid, w_mid, preferred_element_type=F32), PX)
+        above = fold(jnp.dot(both(TW, PX, pair), wc[l, 0 : 2 * CH, :], preferred_element_type=F32), rows3)
+        below = fold(
+            jnp.dot(both(2 * TW, TW + PX, slice(0, 3 * CH)), wc[l, 6 * CH : 9 * CH, :], preferred_element_type=F32), rows3
+        )
+        blank = jnp.zeros((TW, CH), F32)
+        pre = full + jnp.concatenate([blank, above], axis=0) + jnp.concatenate([below, blank], axis=0)
         new = (v + STEP * jnp.tanh(pre + bias[pl.ds(l, 1), :])) * mask[...]
         pad[LAY : LAY + PX, :] = new
         return new
@@ -343,12 +354,34 @@
     my_shard = (z // 2, pl.ds(pl.multiple_of(SH * (z % 2), LAY), SH))
 
     for i in range(CYCLES):
-        lax.fori_loop(0, LAY, plain, 0)
+        if i == 0:
+            lax.fori_loop(0, 2, plain, 0)
+            hear(2)
+            tell(3)
+            lax.fori_loop(2, 4, plain, 0)
+            hear(3)
+            for k in (4, 3, 5, 2, 6, 1, 7):
+                p_copy(k).start()
+            lax.fori_loop(4, LAY, plain, 0)
+        else:
+            lax.fori_loop(0, LAY, plain, 0)
         cc[i] = core(pad[LAY : LAY + PX, :])
         shift_send(i)
         if i == 0:
             for k in range(1, Z):
                 p_copy(k).wait()
+            for k in (2, 1, 3):
+                y_copy(k).start()
+        shift_wait(i)
+        set_start(st[i])
+        lax.fori_loop(0, LAY, plain, 0)
+        rs[i] = core(pad[LAY : LAY + PX, :]) - cc[i]
+        for k in (4, 3, 5, 2, 6, 1, 7):
+            a_copy(i, k).start()
+        rz[i, z] = rs[i, my_shard[0], my_shard[1], :]
+        if i == 0:
+            for k in range(1, 4):
+                y_copy(k).wait()
             forward = remote(pz.at[:, hrows, :], pz.at[:, hrows, :], s_pf.at[0], r_pf.at[0], at(sec, 1 - r, c))
             forward.start()
             forward.wait()
@@ -368,23 +401,6 @@
             mown[...] = prefix
             for k in range(1, X):
                 m_copy(k).start()
-        shift_wait(i)
-        set_start(st[i])
-        lax.fori_loop(0, LAY, plain, 0)
-        rs[i] = core(pad[LAY : LAY + PX, :]) - cc[i]
-        for k in (4, 3, 5, 2, 6, 1, 7):
-            a_copy(i, k).start()
-        rz[i, z] = rs[i, my_shard[0], my_shard[1], :]
-        if i == 0:
-            for k in range(1, X):
-                m_copy(k).wait()
-            near = mx[jnp.maximum(x - 1, 0)]
-            far = mx[jnp.maximum(x - 2, 0)]
-            near = jnp.where(x >= 2, near, 0.0)
-            far = jnp.where(x >= 3, far, 0.0)
-            near_pair = paired(near)
-            nc[0:CH, :] = near_pair
-            nc[CH : 2 * CH, :] = paired(times(far, near_pair))
         for k in range(1, Z):
             a_copy(i, k).wait()
         joined = jnp.concatenate([rz[i, k] for k in range(Z)], axis=1)
@@ -396,6 +412,16 @@
         for k in range(1, Z - 1):
             run = times(run, pc[k]) + rz[i, k]
             local.append(run)
+        if i == 0:
+            for k in range(1, X):
+                m_copy(k).wait()
+            near = mx[jnp.maximum(x - 1, 0)]
+            far = mx[jnp.maximum(x - 2, 0)]
+            near = jnp.where(x >= 2, near, 0.0)
+            far = jnp.where(x >= 3, far, 0.0)
+            near_pair = paired(near)
+            nc[0:CH, :] = near_pair
+            nc[CH : 2 * CH, :] = paired(times(far, near_pair))
         for k in range(1, X):
             t_copy(i, k).wait()
         before = [jnp.where(x >= d, tx[i, jnp.maximum(x - d, 0)], 0.0) for d in range(1, X)]
@@ -426,6 +452,11 @@
             part = dp.at[i, row, pl.ds(0 if side == 0 else TW - LAY, LAY), :]
             return remote(part, part, s_h.at[i, 0], r_h.at[i, side, row], at(sec, 1 - r, c))
 
+        if i == CYCLES - 1:
+            before = dp[i, :, pl.ds(LAY, TC), :].reshape(H * TC, CH)
+            delta = times(before, paired(psum[...])).reshape(H, TC, CH) + rs[i]
+            outb[LAY - 1] = cc[i] + delta
+
         @pl.when(has_left)
         def _():
             for row in range(H):
@@ -458,9 +489,6 @@
             outb.at[l, pl.ds(2 * (1 - r), 2)], out.at[l, 0, :, out_cols, :], s_o.at[l], r_o.at[l], at(sec, 1 - r, c)
         )
 
-    i = CYCLES - 1
-    delta = times(dp[i, :, pl.ds(LAY, TC), :].reshape(H * TC, CH), paired(psum[...])).reshape(H, TC, CH) + rs[i]
-    outb[LAY - 1] = cc[i] + delta
     keep(LAY - 1).start()
     give(LAY - 1).start()
 
@@ -518,6 +546,7 @@
             D((3,)), D((5,)), D((LAY,)), D((n, 3)), D((n, 3)), D((Z,)), D((Z,)), D((1,)), D((1,)),
             D((X,)), D((X,)), D((n, Z)), D((n, Z)), D((n, X)), D((n, X)), D((n, Z)), D((n, Z)),
             D((n, Z)), D((n, 2, H)), D((LAY,)), D((LAY,)), D((LAY,)), D((2,)),
+            D((4,)), D((4,)), pltpu.SemaphoreType.REGULAR((4,)),
         ],
         compiler_params=pltpu.CompilerParams(
             collective_id=0, has_side_effects=True, vmem_limit_bytes=63000000

time: 79.1 us -> 76.8 us (0.971)
  Pallas kernels: 76.9 us -> 74.6 us
    pallas_call x1, Pallas kernels: 76.9 us -> 74.6 us  [shards(): pl.pallas_call(kernel, out_shape=jax.ShapeDtypeStruct((LAY,) + inputs.sha...]
where the time goes in v2:
time: 76.8 us; the launch traced here: 76.7 us
  Pallas kernels  74.6 us (97%)
  local copies, waits for them, and re-layouts  2.07 us (3%)
    pallas_call x1, Pallas kernels, shards(): pl.pallas_call(kernel, out_shape=jax.ShapeDtypeStruct((LAY,) + inputs.sha...  74.6 us
    unnamed x1, local copies, waits for them, and re-layouts  2.07 us

profile of v2, /device:TPU:1, one launch (start us, length us, event | category | flops | bytes accessed | tf_op | source)
XLA Modules:
  0.0 76.7 jit_solution(4045538262262068077)
XLA Ops:
  0.0 74.6 %shard_map.37 = f32[8,1,2,96,128]{4,3,2,1,0:T(8,128)} custom-call(f32[1,2,96,128]{3,2,1,0:T(8,128)} %inp.1, f32[8,9,128,128]{3,2,1,0:T(8,128)} %wts.1, f32[8,128]{1,0:T(8,128)} %bias_in.1), custom_call_target="tpu_custom_call" | custom-call | tf_op jit(solution)/shard_map/pallas_call | solution.py:511
  74.7 2.1 %copy.5 = f32[8,1,2,96,128]{4,3,2,1,0:T(8,128)} copy(f32[8,1,2,96,128]{4,3,2,1,0:T(8,128)} %shard_map.37) | data formatting | bytes 1572864

commit v3 on v2

--- a/solution.py
+++ b/solution.py
@@ -42,7 +42,7 @@
 
 def kernel(
     inp, wts, bias_in, out,
-    xin, bias, x0, wf, wc, psum, a_buf, pad, mask, st, cc, rs, rz, bz, dp, tx, tb, pz, mx, mown, pc, qc, sc, nc, outb,
+    xin, bias, x0, wf, wc, wp, beside, psum, a_buf, pad, mask, st, cc, rs, rz, bz, dp, tx, tb, pz, mx, mown, pc, qc, sc, nc, outb,
     s_in, r_in, w_sem, s_sh, r_sh, s_p, r_p, s_pf, r_pf, s_m, r_m, s_a, r_a, s_t, r_t, s_b, r_b,
     s_h, r_h, s_o, r_o, l_o, x_sem, s_y, r_y, rounds,
 ):
@@ -133,6 +133,7 @@
             dp[i, :, TW - LAY : TW, :] = zero_cols
 
     a_buf[...] = jnp.zeros_like(a_buf)
+    beside[...] = jnp.zeros_like(beside)
     pad[...] = jnp.zeros_like(pad)
     psum[...] = jnp.zeros_like(psum)
     column = lax.broadcasted_iota(jnp.int32, (H, TW, CH), 1)
@@ -145,11 +146,14 @@
         for k in range(9):
             w = wf[l, k]
             total = total + w
-            wc[l, k * CH : (k + 1) * CH, :] = paired(w)
+            duo = paired(w)
+            wc[l, k * CH : (k + 1) * CH, :] = duo
+            row, left = ((k % 3, k < 3), (3 + min(k % 3, 1), k < 5))[k // 3 == 1]
+            wp[l, row * CH : (row + 1) * CH, (0 if left else CH) : (CH if left else 2 * CH)] = duo[:, :CH]
+        wp[l, 3 * CH : 4 * CH, CH:] = jnp.zeros((CH, CH), BF16)
         psum[...] = total
         return carry
 
-    lax.fori_loop(0, 3, convert, 0)
     load_x.wait()
     load_b.wait()
     pl.semaphore_wait(bar, len(around) + 1 + 2 * sides)
@@ -192,10 +196,10 @@
 
     tell(0)
     x0[half, mine, :] = xin[:, src_mine, :]
-    lax.fori_loop(3, 5, convert, 0)
+    lax.fori_loop(0, 4, convert, 0)
     hear(0)
     tell(1)
-    lax.fori_loop(5, LAY, convert, 0)
+    lax.fori_loop(4, LAY, convert, 0)
     rows_i = lax.broadcasted_iota(jnp.int32, (CH, CH), 0)
     cols_i = lax.broadcasted_iota(jnp.int32, (CH, CH), 1)
     eye = jnp.where(rows_i == cols_i, 1.0, 0.0).astype(F32)
@@ -239,20 +243,24 @@
             high, low = split(pad[LAY - 1 + d : LAY - 1 + d + PX, :])
             a_buf[0, TW : TW + PX, d * CH : (d + 1) * CH] = high.astype(BF16)
             a_buf[1, TW : TW + PX, d * CH : (d + 1) * CH] = low.astype(BF16)
-        def both(lo, hi, cols):
-            return jnp.concatenate([a_buf[h, lo:hi, cols] for h in range(2)], axis=0)
-
         rows3 = PX - TW
         pair, third = slice(0, 2 * CH), slice(2 * CH, 3 * CH)
-        mid = jnp.concatenate(
-            [both(TW, TW + PX, pair), both(TW, TW + PX, third), both(0, PX, third)], axis=1
-        )
+        image, upper = slice(TW, TW + PX), slice(0, PX)
+
+        def dot(a, b):
+            return jnp.dot(a, b, preferred_element_type=F32)
+
+        def flat(r):
+            return r[:, :CH] + r[:, CH:]
+
+        low_rows = dot(a_buf[1, image, :], wp[l, 0 : 3 * CH, :])
+        low_mid = dot(a_buf[1, image, pair], wp[l, 3 * CH : 5 * CH, :])
+        beside[0:PX, :] = low_mid[:, CH:]
+        mid = jnp.concatenate([a_buf[0, image, pair], a_buf[0, image, third], a_buf[0, upper, third]], axis=1)
         w_mid = jnp.concatenate([wc[l, 3 * CH : 6 * CH, :], wc[l, 2 * CH : 3 * CH, :]], axis=0)
-        full = fold(jnp.dot(mid, w_mid, preferred_element_type=F32), PX)
-        above = fold(jnp.dot(both(TW, PX, pair), wc[l, 0 : 2 * CH, :], preferred_element_type=F32), rows3)
-        below = fold(
-            jnp.dot(both(2 * TW, TW + PX, slice(0, 3 * CH)), wc[l, 6 * CH : 9 * CH, :], preferred_element_type=F32), rows3
-        )
+        full = flat(dot(mid, w_mid)) + low_mid[:, :CH] + beside[1 : PX + 1, :]
+        above = flat(dot(a_buf[0, TW:PX, pair], wc[l, 0 : 2 * CH, :])) + low_rows[:rows3, :CH]
+        below = flat(dot(a_buf[0, 2 * TW : TW + PX, :], wc[l, 6 * CH : 9 * CH, :])) + low_rows[TW:, CH:]
         blank = jnp.zeros((TW, CH), F32)
         pre = full + jnp.concatenate([blank, above], axis=0) + jnp.concatenate([below, blank], axis=0)
         new = (v + STEP * jnp.tanh(pre + bias[pl.ds(l, 1), :])) * mask[...]
@@ -347,8 +355,8 @@
         to = 0 if side == 0 else TW - LAY
         rc = right_rc if side == 0 else left_rc
         return remote(
-            bz.at[i, k, pl.ds(frm, LAY), :], dp.at[i, z // 2, pl.ds(to, LAY), :], s_h.at[i, k], r_h.at[i, side, z // 2],
-            at(x * Z + k, *rc),
+            bz.at[i, (z + k) % Z, pl.ds(frm, LAY), :], dp.at[i, z // 2, pl.ds(to, LAY), :], s_h.at[i, k], r_h.at[i, side, z // 2],
+            at(x * Z + (z + k) % Z, *rc),
         )
 
     my_shard = (z // 2, pl.ds(pl.multiple_of(SH * (z % 2), LAY), SH))
@@ -358,11 +366,10 @@
             lax.fori_loop(0, 2, plain, 0)
             hear(2)
             tell(3)
-            lax.fori_loop(2, 4, plain, 0)
-            hear(3)
             for k in (4, 3, 5, 2, 6, 1, 7):
                 p_copy(k).start()
-            lax.fori_loop(4, LAY, plain, 0)
+            lax.fori_loop(2, LAY, plain, 0)
+            hear(3)
         else:
             lax.fori_loop(0, LAY, plain, 0)
         cc[i] = core(pad[LAY : LAY + PX, :])
@@ -431,18 +438,18 @@
         spread = jnp.dot(jnp.concatenate([high, low], axis=0).astype(BF16), qc[...], preferred_element_type=F32)
         for k in range(1, Z):
             bz[i, k] = local[k - 1] + fold(spread[:, 2 * CH * (k - 1) : 2 * CH * k], SH)
+        @pl.when((z % 2 == 1) & has_right)
+        def _():
+            for k in (4, 3, 5, 2, 6, 1, 7, 0):
+                h_copy(i, k, 0).start()
+
+        @pl.when((z % 2 == 0) & has_left)
+        def _():
+            for k in (4, 3, 5, 2, 6, 1, 7, 0):
+                h_copy(i, k, 1).start()
+
         for k in (4, 3, 5, 2, 6, 1, 7):
             b_copy(i, k).start()
-
-        @pl.when((z % 2 == 1) & has_right)
-        def _():
-            for k in range(Z):
-                h_copy(i, k, 0).start()
-
-        @pl.when((z % 2 == 0) & has_left)
-        def _():
-            for k in range(Z):
-                h_copy(i, k, 1).start()
 
         dp[i, z // 2, my_cols, :] = bz[i, z]
         for k in range(1, Z):
@@ -523,6 +530,8 @@
             V((H, TW, CH), F32),
             V((LAY, 9, CH, CH), F32),
             V((LAY, 9 * CH, 2 * CH), BF16),
+            V((LAY, 5 * CH, 2 * CH), BF16),
+            V((PX + LAY, CH), F32),
             V((CH, CH), F32),
             V((2, PX + 2 * TW, 3 * CH), BF16),
             V((PX + 2 * LAY, CH), F32),
@@ -549,9 +558,9 @@
             D((4,)), D((4,)), pltpu.SemaphoreType.REGULAR((4,)),
         ],
         compiler_params=pltpu.CompilerParams(
-            collective_id=0, has_side_effects=True, vmem_limit_bytes=63000000
+            collective_id=0, has_side_effects=True, vmem_limit_bytes=54000000
         ),
-    )(inputs, weights, biases)
+    )(pltpu.with_memory_space_constraint(inputs, pltpu.HBM), weights, pltpu.with_memory_space_constraint(biases, pltpu.HBM))
 
 
 def solution(mesh):

time: 76.8 us -> 72.4 us (0.943)
  Pallas kernels: 74.6 us -> 71.5 us
  local copies, waits for them, and re-layouts: 2.07 us -> 0.88 us
    pallas_call x1, Pallas kernels: 74.6 us -> 71.5 us  [shards(): pl.pallas_call(kernel, out_shape=jax.ShapeDtypeStruct((LAY,) + inputs.sha...]
    unnamed x1, local copies, waits for them, and re-layouts: 2.07 us -> 0.88 us
where the time goes in v3:
time: 72.4 us; the launch traced here: 72.3 us
  Pallas kernels  71.5 us (99%)
  local copies, waits for them, and re-layouts  0.88 us (1%)
    pallas_call x1, Pallas kernels, shards(): pl.pallas_call(kernel, out_shape=jax.ShapeDtypeStruct((LAY,) + inputs.sha...  71.5 us

profile of v3, /device:TPU:1, one launch (start us, length us, event | category | flops | bytes accessed | tf_op | source)
XLA Modules:
  0.0 72.3 jit_solution(15115800708391378921)
XLA Ops:
  0.0 71.5 %shard_map.37 = f32[8,1,2,96,128]{4,3,2,1,0:T(8,128)S(1)} custom-call(f32[1,2,96,128]{3,2,1,0:T(8,128)} %inp.1, f32[8,9,128,128]{3,2,1,0:T(8,128)} %wts.1, f32[8,128]{1,0:T(8,128)} %bias_in.1), custom_call_target="tpu_custom_call" | custom-call | tf_op jit(solution)/shard_map/pallas_call | solution.py:518
  71.5 0.9 %copy.5 = f32[8,1,2,96,128]{4,3,2,1,0:T(8,128)} copy(f32[8,1,2,96,128]{4,3,2,1,0:T(8,128)S(1)} %shard_map.37) | data formatting | bytes 1572864

commit v4 on v3

--- a/solution.py
+++ b/solution.py
@@ -339,7 +339,7 @@
     def a_copy(i, k):
         j = (z + k) % Z
         part = rs.at[i, j // 2, pl.ds(pl.multiple_of(SH * (j % 2), LAY), SH), :]
-        return remote(part, rz.at[i, z], s_a.at[i, k], r_a.at[i, k], at(x * Z + j, r, c))
+        return remote(part, rz.at[i, z], s_a.at[i, k], r_a.at[i, k], at(x * Z + j, 1 - r, c))
 
     def t_copy(i, k):
         return remote(tb.at[i], tx.at[i, x], s_t.at[i, k], r_t.at[i, k], at(((x + k) % X) * Z + z, r, c))
@@ -348,18 +348,20 @@
 
     def b_copy(i, k):
         j = (z + k) % Z
-        return remote(bz.at[i, j], dp.at[i, z // 2, my_cols, :], s_b.at[i, k], r_b.at[i, k], at(x * Z + j, r, c))
+        return remote(bz.at[i, j], dp.at[i, z // 2, my_cols, :], s_b.at[i, k], r_b.at[i, k], at(x * Z + j, 1 - r, c))
 
     def h_copy(i, k, side):
         frm = (SH - LAY) if side == 0 else 0
         to = 0 if side == 0 else TW - LAY
-        rc = right_rc if side == 0 else left_rc
+        rc = (r, c + 1 - r) if side == 0 else (r, c - r)
         return remote(
             bz.at[i, (z + k) % Z, pl.ds(frm, LAY), :], dp.at[i, z // 2, pl.ds(to, LAY), :], s_h.at[i, k], r_h.at[i, side, z // 2],
             at(x * Z + (z + k) % Z, *rc),
         )
 
-    my_shard = (z // 2, pl.ds(pl.multiple_of(SH * (z % 2), LAY), SH))
+    odd = z % 2 == 1
+    own_right, own_left = odd & (2 * c + 1 - r < last), (z % 2 == 0) & (2 * c + 1 - r > 0)
+    inner_right, inner_left = odd & (r == 1), (z % 2 == 0) & (r == 0)
 
     for i in range(CYCLES):
         if i == 0:
@@ -383,9 +385,8 @@
         set_start(st[i])
         lax.fori_loop(0, LAY, plain, 0)
         rs[i] = core(pad[LAY : LAY + PX, :]) - cc[i]
-        for k in (4, 3, 5, 2, 6, 1, 7):
+        for k in (4, 3, 5, 2, 6, 1, 7, 0):
             a_copy(i, k).start()
-        rz[i, z] = rs[i, my_shard[0], my_shard[1], :]
         if i == 0:
             for k in range(1, 4):
                 y_copy(k).wait()
@@ -408,7 +409,7 @@
             mown[...] = prefix
             for k in range(1, X):
                 m_copy(k).start()
-        for k in range(1, Z):
+        for k in range(Z):
             a_copy(i, k).wait()
         joined = jnp.concatenate([rz[i, k] for k in range(Z)], axis=1)
         tb[i] = times(joined, sc[...])
@@ -438,21 +439,28 @@
         spread = jnp.dot(jnp.concatenate([high, low], axis=0).astype(BF16), qc[...], preferred_element_type=F32)
         for k in range(1, Z):
             bz[i, k] = local[k - 1] + fold(spread[:, 2 * CH * (k - 1) : 2 * CH * k], SH)
-        @pl.when((z % 2 == 1) & has_right)
-        def _():
-            for k in (4, 3, 5, 2, 6, 1, 7, 0):
-                h_copy(i, k, 0).start()
-
-        @pl.when((z % 2 == 0) & has_left)
-        def _():
-            for k in (4, 3, 5, 2, 6, 1, 7, 0):
-                h_copy(i, k, 1).start()
-
-        for k in (4, 3, 5, 2, 6, 1, 7):
+        for side, sends, inner in ((0, own_right, inner_right), (1, own_left, inner_left)):
+            @pl.when(sends)
+            def _():
+                for k in (4, 3, 5, 2, 6, 1, 7):
+                    h_copy(i, k, side).start()
+
+                @pl.when(jnp.logical_not(inner))
+                def _():
+                    h_copy(i, 0, side).start()
+
+        for k in (4, 3, 5, 2, 6, 1, 7, 0):
             b_copy(i, k).start()
 
-        dp[i, z // 2, my_cols, :] = bz[i, z]
-        for k in range(1, Z):
+        @pl.when(inner_right)
+        def _():
+            dp[i, z // 2, 0:LAY, :] = bz[i, z, SH - LAY : SH, :]
+
+        @pl.when(inner_left)
+        def _():
+            dp[i, z // 2, TW - LAY : TW, :] = bz[i, z, 0:LAY, :]
+
+        for k in range(Z):
             b_copy(i, k).wait()
 
         def halo_in(side, row):
@@ -464,25 +472,23 @@
             delta = times(before, paired(psum[...])).reshape(H, TC, CH) + rs[i]
             outb[LAY - 1] = cc[i] + delta
 
-        @pl.when(has_left)
-        def _():
-            for row in range(H):
-                halo_in(0, row).wait_recv()
-
-        @pl.when(has_right)
-        def _():
-            for row in range(H):
-                halo_in(1, row).wait_recv()
-
-        @pl.when((z % 2 == 1) & has_right)
-        def _():
-            for k in range(Z):
-                h_copy(i, k, 0).wait_send()
-
-        @pl.when((z % 2 == 0) & has_left)
-        def _():
-            for k in range(Z):
-                h_copy(i, k, 1).wait_send()
+        for side, comes, inner in ((0, has_left, inner_right), (1, has_right, inner_left)):
+            @pl.when(comes)
+            def _():
+                for row in range(H):
+                    @pl.when(jnp.logical_not(inner & (z // 2 == row)))
+                    def _():
+                        halo_in(side, row).wait_recv()
+
+        for side, sends, inner in ((0, own_right, inner_right), (1, own_left, inner_left)):
+            @pl.when(sends)
+            def _():
+                for k in range(1, Z):
+                    h_copy(i, k, side).wait_send()
+
+                @pl.when(jnp.logical_not(inner))
+                def _():
+                    h_copy(i, 0, side).wait_send()
 
         set_start(st[i] + dp[i])
 

time: 72.4 us -> 71.4 us (0.986)
  Pallas kernels: 71.5 us -> 70.4 us
    pallas_call x1, Pallas kernels: 71.5 us -> 70.4 us  [shards(): pl.pallas_call(kernel, out_shape=jax.ShapeDtypeStruct((LAY,) + inputs.sha...]
where the time goes in v4:
time: 71.4 us; the launch traced here: 71.3 us
  Pallas kernels  70.4 us (99%)
  local copies, waits for them, and re-layouts  0.88 us (1%)
    pallas_call x1, Pallas kernels, shards(): pl.pallas_call(kernel, out_shape=jax.ShapeDtypeStruct((LAY,) + inputs.sha...  70.4 us

profile of v4, /device:TPU:1, one launch (start us, length us, event | category | flops | bytes accessed | tf_op | source)
XLA Modules:
  0.0 71.3 jit_solution(9292263035603491950)
XLA Ops:
  0.0 70.4 %shard_map.37 = f32[8,1,2,96,128]{4,3,2,1,0:T(8,128)S(1)} custom-call(f32[1,2,96,128]{3,2,1,0:T(8,128)} %inp.1, f32[8,9,128,128]{3,2,1,0:T(8,128)} %wts.1, f32[8,128]{1,0:T(8,128)} %bias_in.1), custom_call_target="tpu_custom_call" | custom-call | tf_op jit(solution)/shard_map/pallas_call | solution.py:524
  70.4 0.9 %copy.5 = f32[8,1,2,96,128]{4,3,2,1,0:T(8,128)} copy(f32[8,1,2,96,128]{4,3,2,1,0:T(8,128)S(1)} %shard_map.37) | data formatting | bytes 1572864

commit v5 on v4

--- a/solution.py
+++ b/solution.py
@@ -272,8 +272,9 @@
 
     set_start(x0[...])
 
-    def plain(l, carry):
-        layer(l)
+    def double(m, carry):
+        layer(2 * m)
+        layer(2 * m + 1)
         return carry
 
     def shift(i):
@@ -365,15 +366,15 @@
 
     for i in range(CYCLES):
         if i == 0:
-            lax.fori_loop(0, 2, plain, 0)
+            double(0, 0)
             hear(2)
             tell(3)
             for k in (4, 3, 5, 2, 6, 1, 7):
                 p_copy(k).start()
-            lax.fori_loop(2, LAY, plain, 0)
+            lax.fori_loop(1, LAY // 2, double, 0)
             hear(3)
         else:
-            lax.fori_loop(0, LAY, plain, 0)
+            lax.fori_loop(0, LAY // 2, double, 0)
         cc[i] = core(pad[LAY : LAY + PX, :])
         shift_send(i)
         if i == 0:
@@ -383,7 +384,7 @@
                 y_copy(k).start()
         shift_wait(i)
         set_start(st[i])
-        lax.fori_loop(0, LAY, plain, 0)
+        lax.fori_loop(0, LAY // 2, double, 0)
         rs[i] = core(pad[LAY : LAY + PX, :]) - cc[i]
         for k in (4, 3, 5, 2, 6, 1, 7, 0):
             a_copy(i, k).start()
@@ -407,8 +408,10 @@
                 if back > 0:
                     suffix = times(pz[back], pair)
             mown[...] = prefix
-            for k in range(1, X):
-                m_copy(k).start()
+            for k in range(1, X - 1):
+                @pl.when((x >= 1) & (x + k < X))
+                def _():
+                    m_copy(k).start()
         for k in range(Z):
             a_copy(i, k).wait()
         joined = jnp.concatenate([rz[i, k] for k in range(Z)], axis=1)
@@ -421,8 +424,14 @@
             run = times(run, pc[k]) + rz[i, k]
             local.append(run)
         if i == 0:
-            for k in range(1, X):
-                m_copy(k).wait()
+            for k in range(1, X - 1):
+                @pl.when((x >= 1) & (x + k < X))
+                def _():
+                    m_copy(k).wait_send()
+
+                @pl.when(x - k >= 1)
+                def _():
+                    m_copy(k).wait_recv()
             near = mx[jnp.maximum(x - 1, 0)]
             far = mx[jnp.maximum(x - 2, 0)]
             near = jnp.where(x >= 2, near, 0.0)
@@ -511,7 +520,11 @@
         give(l).start()
         return carry
 
-    lax.fori_loop(0, LAY - 1, final, 0)
+    def last_two(m, carry):
+        return final(2 * m + 1, final(2 * m, carry))
+
+    lax.fori_loop(0, LAY // 2 - 1, last_two, 0)
+    final(LAY - 2, 0)
     for l in range(LAY):
         keep(l).wait()
         give(l).wait()

time: 71.4 us -> 71 us (level)
  no operation moved by 1% of the time
where the time goes in v5:
time: 71 us; the launch traced here: 70.9 us
  Pallas kernels  70 us (99%)
  local copies, waits for them, and re-layouts  0.88 us (1%)
    pallas_call x1, Pallas kernels, shards(): pl.pallas_call(kernel, out_shape=jax.ShapeDtypeStruct((LAY,) + inputs.sha...  70 us

profile of v5, /device:TPU:1, one launch (start us, length us, event | category | flops | bytes accessed | tf_op | source)
XLA Modules:
  0.0 70.9 jit_solution(16880844089735502202)
XLA Ops:
  0.0 70.0 %shard_map.37 = f32[8,1,2,96,128]{4,3,2,1,0:T(8,128)S(1)} custom-call(f32[1,2,96,128]{3,2,1,0:T(8,128)} %inp.1, f32[8,9,128,128]{3,2,1,0:T(8,128)} %wts.1, f32[8,128]{1,0:T(8,128)} %bias_in.1), custom_call_target="tpu_custom_call" | custom-call | tf_op jit(solution)/shard_map/pallas_call | solution.py:537
  70.0 0.9 %copy.5 = f32[8,1,2,96,128]{4,3,2,1,0:T(8,128)} copy(f32[8,1,2,96,128]{4,3,2,1,0:T(8,128)S(1)} %shard_map.37) | data formatting | bytes 1572864
